TPU v7x, 32 devices: a whole 2x2x4 slice. The times are simulated.
32 devices in a mesh: grp: 2 (over y), smp: 4 (over z), trm: 2 (over x), sub: 2 (over core).
Axes of the slice: x: 2, y: 2, z: 4, core: 2. Of those that a mesh axis runs over, the one named last changes fastest.
Arguments:
- inputs: float32 [20, 8192], P(None, ('grp', 'smp', 'sub')), parts along dimension 1, may hold values from -1 to 1
- weights: float32 [8192], P(('grp', 'smp', 'sub')), parts along dimension 0, may hold values from 0.25 to 4
- response: float32 [8192], P(('grp', 'smp', 'sub')), parts along dimension 0, may hold values from 0.5 to 3
- index_table: int32 [20, 1792], P(None, 'trm'), may hold values from 0 to 3, as said below
Outputs:
- gram: float32 [3584, 1792], P(('grp', 'trm'), ('smp', 'sub')), parts along dimension 0
- rhs: float32 [3584], P(('grp', 'trm')), parts along dimension 0
There are 2 independent parts, one for each index of `grp`. A program takes and returns all parts, laid end to end along the dimension named above; an argument that names none is the same for every part. Nothing has to cross between parts.
Inputs may be any that keep to these rules, and one draw needn't show every extreme that they name: `index_table`: each column holds the degrees of a multi-index of total degree at most 3. No multi-index other than the all-zero one stands in two columns; when 1792 is 1771 or more, every multi-index of total degree at most 3 over 20 inputs stands in some column.
All inputs are finite; a program needn't handle non-finite values.
Results may differ from a plain program's by a relative error of at most 0.00043.
Values may be sent and summed in bfloat16 or wider, within the bound.
A program may use at most 64 MiB of HBM per device.

v0:
```python
import functools

import jax
import jax.numpy as jnp
from jax import lax
from jax.experimental import pallas as pl
from jax.experimental.pallas import tpu as pltpu
from jax.sharding import PartitionSpec as P

MESH = pl.DeviceIdType.MESH


def up8(n):
    return -(-n // 8) * 8


class Plan:
    def __init__(self, nin):
        self.nin = nin
        self.single = up8(nin + 1)
        self.slab = up8(nin + 2)
        self.pairs = up8(nin * (nin - 1) // 2)
        self.triple = {}
        row = 0
        for c in range(2, nin + 1):
            self.triple[c] = row
            row += up8(c * (c - 1) // 2)
        self.square = row
        row += nin * self.single
        self.linear = row
        row += self.single
        self.cube = row
        row += self.single
        self.rows = -(-row // 16) * 16


def positions(plan, degrees):
    total = jnp.zeros_like(degrees[0:1, :])
    first, second, third = total, total, total
    for j in range(plan.nin):
        total = total + degrees[j : j + 1, :]
        first = first + (total < 1).astype(jnp.int32)
        second = second + (total < 2).astype(jnp.int32)
        third = third + (total < 3).astype(jnp.int32)
    nin, single = plan.nin, plan.single
    offset = jnp.zeros_like(total)
    for c, start in plan.triple.items():
        offset = jnp.where(third == c, start, offset)
    code = offset + (second * (second - 1)) // 2 + first
    code = jnp.where(
        (first == second) & (second < third), plan.square + first * single + third, code
    )
    code = jnp.where(
        (first < second) & (second == third), plan.square + second * single + first, code
    )
    code = jnp.where((first == second) & (second == third), plan.cube + first, code)
    return jnp.where((second == nin) & (third == nin), plan.linear + first, code)


def build_left(plan, slab, q_ref, pair_ref, left_ref):
    nin, single = plan.nin, plan.single
    x = slab[0:single, :]
    root = slab[nin : nin + 1, :]
    rows = lax.broadcasted_iota(jnp.int32, x.shape, 0)
    q1 = jnp.where(rows < nin, jnp.sqrt(jnp.float32(3.0)) * x, (rows == nin).astype(jnp.float32))
    q2 = jnp.sqrt(jnp.float32(5.0)) * (1.5 * x * x - 0.5) * root
    q3 = jnp.sqrt(jnp.float32(7.0)) * (2.5 * x * x * x - 1.5 * x) * root
    q1_root = q1 * root
    q_ref[0:single, :] = q1
    q_ref[single : 2 * single, :] = q2
    for b in range(1, nin):
        at = b * (b - 1) // 2
        pair_ref[at : at + b, :] = q1_root[0:b, :] * q1[b : b + 1, :]
    blocks = []
    for c in range(2, nin + 1):
        for r in range(0, up8(c * (c - 1) // 2), 8):
            blocks.append(("pair", r, c))
    for c in range(nin):
        for r in range(0, single, 8):
            blocks.append(("one", r, c))
    for r in range(0, single, 8):
        blocks.append(("lin", r, 0))
    for r in range(0, single, 8):
        blocks.append(("cube", r, 0))

    def value(kind, r, c):
        if kind == "pair":
            v = pair_ref[r : r + 8, :]
            return v if c == nin else v * q_ref[c : c + 1, :]
        if kind == "one":
            return q_ref[r : r + 8, :] * q_ref[single + c : single + c + 1, :]
        return (q1_root if kind == "lin" else q3)[r : r + 8, :]

    for g in range(0, len(blocks), 2):
        low = value(*blocks[g])
        high = value(*blocks[g + 1]) if g + 1 < len(blocks) else jnp.zeros_like(low)
        left_ref[8 * g : 8 * g + 16, :] = jnp.concatenate([low, high], axis=0).astype(jnp.bfloat16)


def xor_index(a, b, n):
    if n & (n - 1):
        return lax.rem(a + b, n)
    out, bit = 0, 1
    while bit < n:
        out = out + bit * (((a // bit) % 2 + (b // bit) % 2) % 2)
        bit *= 2
    return out


def kernel(
    plan, sizes, columns, samples_total,
    x_ref, w_ref, y_ref, deg_ref, gram_ref, rhs_ref,
    slabs, code_ref, codes_in, code_smem, sel_ref, left_a, left_b, q_ref, pair_ref, acc, picked,
    ici_send, sub_send, recv, code_send, code_recv, smem_sem,
):
    nsmp, nsub, ntrm = sizes
    smp, sub, trm = lax.axis_index("smp"), lax.axis_index("sub"), lax.axis_index("trm")
    me = smp * nsub + sub
    single = plan.single
    terms = deg_ref.shape[1]
    width = acc.shape[1]

    barrier = pltpu.get_barrier_semaphore()
    for d in range(1, nsmp):
        pl.semaphore_signal(barrier, inc=1, device_id={"smp": xor_index(smp, d, nsmp)}, device_id_type=MESH)
    for d in range(1, nsub):
        pl.semaphore_signal(barrier, inc=1, device_id={"sub": lax.rem(sub + d, nsub)}, device_id_type=MESH)
    for d in range(1, ntrm):
        pl.semaphore_signal(barrier, inc=1, device_id={"trm": lax.rem(trm + d, ntrm)}, device_id_type=MESH)

    weights = w_ref[...]
    root = jnp.sqrt(weights / samples_total)
    scaled = (weights * y_ref[...] / samples_total).astype(jnp.bfloat16).astype(jnp.float32)
    mine = slabs.at[me]
    spare = plan.slab - plan.nin - 2
    mine[...] = jnp.concatenate(
        [x_ref[...], root, scaled / root, jnp.zeros((spare, x_ref.shape[1]), jnp.float32)], axis=0
    )
    code = positions(plan, deg_ref[...])
    code_ref[...] = code
    per_trm = terms // columns
    for k in range(per_trm):
        @pl.when(lax.rem(me, per_trm) == k)
        def _():
            part = code[:, k * columns : (k + 1) * columns].astype(jnp.float32)
            pad = jnp.full((1, width - columns), -1.0, jnp.float32)
            codes_in[trm] = jnp.broadcast_to(jnp.concatenate([part, pad], axis=1), (8, width))
    to_smem = pltpu.make_async_copy(code_ref, code_smem, smem_sem)
    to_smem.start()
    pair_ref[...] = jnp.zeros_like(pair_ref)
    acc[...] = jnp.zeros_like(acc)

    pl.semaphore_wait(barrier, (nsmp - 1) + (nsub - 1) + (ntrm - 1))

    def sub_copy(chunk, p, d):
        return pltpu.make_async_remote_copy(
            src_ref=slabs.at[chunk], dst_ref=slabs.at[chunk],
            send_sem=sub_send.at[p, d - 1], recv_sem=recv.at[chunk],
            device_id={"sub": lax.rem(sub + d, nsub)}, device_id_type=MESH,
        )

    def ici_copy(d):
        return pltpu.make_async_remote_copy(
            src_ref=slabs.at[me], dst_ref=slabs.at[me],
            send_sem=ici_send.at[d - 1], recv_sem=recv.at[me],
            device_id={"smp": xor_index(smp, d, nsmp)}, device_id_type=MESH,
        )

    def code_copy(d):
        return pltpu.make_async_remote_copy(
            src_ref=codes_in.at[trm], dst_ref=codes_in.at[trm],
            send_sem=code_send.at[d - 1], recv_sem=code_recv.at[trm],
            device_id={"trm": lax.rem(trm + d, ntrm)}, device_id_type=MESH,
        )

    def wait_slab(chunk):
        pltpu.make_async_remote_copy(
            src_ref=slabs.at[chunk], dst_ref=slabs.at[chunk],
            send_sem=ici_send.at[0], recv_sem=recv.at[chunk],
            device_id={"sub": lax.rem(sub + 1, nsub)}, device_id_type=MESH,
        ).wait_recv()

    for d in range(1, ntrm):
        code_copy(d).start()
    for d in range(1, nsub):
        sub_copy(me, 0, d).start()
    for d in range(1, nsmp):
        ici_copy(d).start()

    build_left(plan, slabs[me], q_ref, pair_ref, left_a)

    for d in range(1, ntrm):
        other = lax.rem(trm + d, ntrm)
        pltpu.make_async_remote_copy(
            src_ref=codes_in.at[other], dst_ref=codes_in.at[other],
            send_sem=code_send.at[d - 1], recv_sem=code_recv.at[other],
            device_id={"trm": other}, device_id_type=MESH,
        ).wait_recv()
    owner = me // per_trm
    wanted = codes_in[owner]
    for i in range(0, width, 128):
        column = jnp.broadcast_to(wanted[0:1, i : i + 128], (128, 128)).T.astype(jnp.int32)
        for j in range(0, sel_ref.shape[1], 128):
            cols = min(128, sel_ref.shape[1] - j)
            lane = lax.broadcasted_iota(jnp.int32, (128, cols), 1) + j
            sel_ref[i : i + 128, j : j + cols] = (column[:, :cols] == lane).astype(jnp.bfloat16)

    def chunk_of(p, s):
        return xor_index(smp, p, nsmp) * nsub + lax.rem(sub + s, nsub)

    def compute(chunk, left_ref):
        left = left_ref[...]
        right = lax.dot_general(
            sel_ref[...], left, (((1,), (0,)), ((), ())), preferred_element_type=jnp.float32
        )
        z = slabs[chunk][plan.nin + 1 : plan.nin + 2, :]
        high = z.astype(jnp.bfloat16).astype(jnp.float32)
        low = z - high
        rows = lax.broadcasted_iota(jnp.int32, right.shape, 0)
        right = jnp.where(rows == columns, high, jnp.where(rows == columns + 1, low, right))
        acc[...] += lax.dot_general(
            left, right.astype(jnp.bfloat16), (((1,), (1,)), ((), ())),
            preferred_element_type=jnp.float32,
        )

    def body(p, carry):
        second = chunk_of(p, 1)
        wait_slab(second)
        compute(chunk_of(p, 0), left_a)
        build_left(plan, slabs[second], q_ref, pair_ref, left_b)
        following = chunk_of(lax.rem(p + 1, nsmp), 0)

        @pl.when(p + 1 < nsmp)
        def _():
            wait_slab(following)
            for d in range(1, nsub):
                sub_copy(following, p + 1, d).start()

        compute(second, left_b)
        build_left(plan, slabs[following], q_ref, pair_ref, left_a)
        return carry

    lax.fori_loop(0, nsmp, body, 0)

    to_smem.wait()

    for base in range(0, terms, 128):
        count = min(128, terms - base)
        for r in range(base, base + count):
            picked[r : r + 1, :] = acc[pl.ds(code_smem[0, r], 1), :]
        turned = picked[base : base + count, :].T
        gram_ref[:, base : base + count] = turned[0:columns, :]
        rhs_ref[:, base : base + count] = (
            turned[columns : columns + 1, :] + turned[columns + 1 : columns + 2, :]
        )

    for d in range(1, ntrm):
        code_copy(d).wait_send()
    for d in range(1, nsmp):
        ici_copy(d).wait_send()
    for p in range(nsmp):
        for d in range(1, nsub):
            sub_copy(chunk_of(p, 0), p, d).wait_send()


def solution(mesh):
    nsmp, nsub, ntrm = mesh.shape["smp"], mesh.shape["sub"], mesh.shape["trm"]

    def local(inputs, weights, response, index_table):
        nin, samples = inputs.shape
        terms = index_table.shape[1]
        columns = terms * ntrm // (nsmp * nsub)
        plan = Plan(nin)
        width = -(-(columns + 2) // 128) * 128
        chunks = nsmp * nsub
        gram, rhs = pl.pallas_call(
            functools.partial(kernel, plan, (nsmp, nsub, ntrm), columns, samples * chunks),
            out_shape=(
                jax.ShapeDtypeStruct((columns, terms), jnp.float32),
                jax.ShapeDtypeStruct((1, terms), jnp.float32),
            ),
            in_specs=[pl.BlockSpec(memory_space=pltpu.VMEM)] * 4,
            out_specs=(pl.BlockSpec(memory_space=pltpu.VMEM),) * 2,
            scratch_shapes=[
                pltpu.VMEM((chunks, plan.slab, samples), jnp.float32),
                pltpu.VMEM((1, terms), jnp.int32),
                pltpu.VMEM((ntrm, 8, width), jnp.float32),
                pltpu.SMEM((1, terms), jnp.int32),
                pltpu.VMEM((width, plan.rows), jnp.bfloat16),
                pltpu.VMEM((plan.rows, samples), jnp.bfloat16),
                pltpu.VMEM((plan.rows, samples), jnp.bfloat16),
                pltpu.VMEM((2 * plan.single, samples), jnp.float32),
                pltpu.VMEM((plan.pairs, samples), jnp.float32),
                pltpu.VMEM((plan.rows, width), jnp.float32),
                pltpu.VMEM((terms, width), jnp.float32),
                pltpu.SemaphoreType.DMA((max(nsmp - 1, 1),)),
                pltpu.SemaphoreType.DMA((nsmp, max(nsub - 1, 1))),
                pltpu.SemaphoreType.DMA((chunks,)),
                pltpu.SemaphoreType.DMA((max(ntrm - 1, 1),)),
                pltpu.SemaphoreType.DMA((ntrm,)),
                pltpu.SemaphoreType.DMA,
            ],
            compiler_params=pltpu.CompilerParams(
                collective_id=0, has_side_effects=True, vmem_limit_bytes=56 * 1024 * 1024
            ),
        )(inputs, weights.reshape(1, samples), response.reshape(1, samples), index_table)
        return gram.T, rhs.reshape(terms)

    return jax.shard_map(
        local,
        mesh=mesh,
        in_specs=(
            P(None, ("grp", "smp", "sub")),
            P(("grp", "smp", "sub")),
            P(("grp", "smp", "sub")),
            P(None, "trm"),
        ),
        out_specs=(P(("grp", "trm"), ("smp", "sub")), P(("grp", "trm"))),
        check_vma=False,
    )
```

profile of v0, /device:TPU:0, one launch (start us, length us, event | category | flops | bytes accessed | tf_op | source)
XLA Modules:
  0.0 33.0 jit_solution(3429333779134248865)
XLA Ops:
  0.6 29.0 %shard_map.59 = (f32[224,896]{1,0:T(8,128)}, f32[1,896]{1,0:T(1,128)}) custom-call(f32[20,512]{1,0:T(8,128)} %x_ref.1, f32[1,512]{1,0:T(1,128)} %bitcast.4, f32[1,512]{1,0:T(1,128)} %bitcast.5, s32[20,896]{1,0:T(8,128)} %deg_ref.1), custom_call_target="tpu_custom_call" | custom-call | tf_op jit(solution)/shard_map/pallas_call | solution.py:276
  29.6 0.0 copy-start
  29.7 0.7 %copy-done = f32[1,896]{1,0:T(1,128)S(1)} copy-done((f32[1,896]{1,0:T(1,128)S(1)}, f32[1,896]{1,0:T(1,128)}, u32[]{:S(2)}) %copy-start) | copy-done | bytes 3608
  30.3 0.6 %reduce = f32[896]{0:T(1024)} reduce(f32[1,896]{1,0:T(1,128)S(1)} %copy-done, f32[]{:T(128)} %constant), dimensions={0}, to_apply=%get-tuple-element.5.reduce_sub_computation | reduce | bytes 7172 | tf_op jit(solution)/shard_map/pallas_call | solution.py:276
  30.9 2.1 %copy.7 = f32[896,224]{0,1:T(8,128)} copy(f32[896,224]{0,1:T(8,128)} %bitcast.3) | data formatting | bytes 1605632
Async XLA Ops:
  29.6 0.7 %copy-start = (f32[1,896]{1,0:T(1,128)S(1)}, f32[1,896]{1,0:T(1,128)}, u32[]{:S(2)}) copy-start(f32[1,896]{1,0:T(1,128)} %get-tuple-element.5) | copy-start | bytes 10756
where the time goes:
time: 33.2 us; the launch traced here: 33 us
  Pallas kernels  29 us (87%)
  local copies, waits for them, and re-layouts  2.74 us (8%)
  between operations  0.65 us (2%)
  other arithmetic  0.61 us (2%)
    pallas_call x1, Pallas kernels, local(): pl.pallas_call(functools.partial(kernel, plan, (nsmp, nsub, ntrm), column...  29 us
    unnamed x3, local copies, waits for them, and re-layouts  2.74 us

commit v1 on v0

--- a/solution.py
+++ b/solution.py
@@ -250,7 +250,7 @@
             picked[r : r + 1, :] = acc[pl.ds(code_smem[0, r], 1), :]
         turned = picked[base : base + count, :].T
         gram_ref[:, base : base + count] = turned[0:columns, :]
-        rhs_ref[:, base : base + count] = (
+        rhs_ref[base // 128 : base // 128 + 1, 0:count] = (
             turned[columns : columns + 1, :] + turned[columns + 1 : columns + 2, :]
         )
 
@@ -261,6 +261,16 @@
     for p in range(nsmp):
         for d in range(1, nsub):
             sub_copy(chunk_of(p, 0), p, d).wait_send()
+
+
+def write_out(gram_ref, rhs_ref, gram_out, rhs_out, flat, sem):
+    copy = pltpu.make_async_copy(gram_ref, gram_out, sem.at[0])
+    copy.start()
+    flat[...] = rhs_ref[...].reshape(flat.shape)
+    line = pltpu.make_async_copy(flat.at[pl.ds(0, rhs_out.shape[0])], rhs_out, sem.at[1])
+    line.start()
+    line.wait()
+    copy.wait()
 
 
 def solution(mesh):
@@ -276,8 +286,8 @@
         gram, rhs = pl.pallas_call(
             functools.partial(kernel, plan, (nsmp, nsub, ntrm), columns, samples * chunks),
             out_shape=(
-                jax.ShapeDtypeStruct((columns, terms), jnp.float32),
-                jax.ShapeDtypeStruct((1, terms), jnp.float32),
+                pltpu.VMEM((columns, terms), jnp.float32),
+                pltpu.VMEM((up8(-(-terms // 128)), 128), jnp.float32),
             ),
             in_specs=[pl.BlockSpec(memory_space=pltpu.VMEM)] * 4,
             out_specs=(pl.BlockSpec(memory_space=pltpu.VMEM),) * 2,
@@ -304,7 +314,23 @@
                 collective_id=0, has_side_effects=True, vmem_limit_bytes=56 * 1024 * 1024
             ),
         )(inputs, weights.reshape(1, samples), response.reshape(1, samples), index_table)
-        return gram.T, rhs.reshape(terms)
+        gram, rhs = pl.pallas_call(
+            write_out,
+            out_shape=(
+                jax.ShapeDtypeStruct((columns, terms), jnp.float32),
+                jax.ShapeDtypeStruct((rhs.size if terms % 128 else terms,), jnp.float32),
+            ),
+            in_specs=[pl.BlockSpec(memory_space=pltpu.VMEM)] * 2,
+            out_specs=(pl.BlockSpec(memory_space=pl.ANY),) * 2,
+            scratch_shapes=[
+                pltpu.VMEM((rhs.size,), jnp.float32),
+                pltpu.SemaphoreType.DMA((2,)),
+            ],
+        )(
+            pltpu.with_memory_space_constraint(gram, pltpu.VMEM),
+            pltpu.with_memory_space_constraint(rhs, pltpu.VMEM),
+        )
+        return gram.T, rhs[0:terms]
 
     return jax.shard_map(
         local,

time: 33.2 us -> 29.8 us (0.90)
  local copies, waits for them, and re-layouts: 2.74 us -> 0 us
  other arithmetic: 0.61 us -> 0 us
    unnamed x3 -> x0, local copies, waits for them, and re-layouts: 2.74 us -> none
    pallas_call x0 -> x1, Pallas kernels: none -> 0.9 us  [local(): pl.pallas_call(write_out, out_shape=(jax.ShapeDtypeStruct((columns, terms...]
    pallas_call x1, Pallas kernels: 29 us -> 28.1 us  [local(): pl.pallas_call(functools.partial(kernel, plan, (nsmp, nsub, ntrm), column...]
    pallas_call x1 -> x0, other arithmetic: 0.61 us -> none  [local(): pl.pallas_call(functools.partial(kernel, plan, (nsmp, nsub, ntrm), column...]
where the time goes in v1:
time: 29.8 us; the launch traced here: 29.7 us
  Pallas kernels  29 us (97%)
  between operations  0.64 us (2%)
    pallas_call x1, Pallas kernels, local(): pl.pallas_call(functools.partial(kernel, plan, (nsmp, nsub, ntrm), column...  28.1 us
    pallas_call x1, Pallas kernels, local(): pl.pallas_call(write_out, out_shape=(jax.ShapeDtypeStruct((columns, terms...  0.9 us

profile of v1, /device:TPU:0, one launch (start us, length us, event | category | flops | bytes accessed | tf_op | source)
XLA Modules:
  0.0 29.7 jit_solution(5209784487234774660)
XLA Ops:
  0.6 28.1 %shard_map.59 = (f32[224,896]{1,0:T(8,128)S(1)}, f32[8,128]{1,0:T(8,128)S(1)}) custom-call(f32[20,512]{1,0:T(8,128)} %x_ref.1, f32[1,512]{1,0:T(1,128)} %bitcast.3, f32[1,512]{1,0:T(1,128)} %bitcast.4, s32[20,896]{1,0:T(8,128)} %deg_ref.1), custom_call_target="tpu_custom_call" | custom-call | tf_op jit(solution)/shard_map/pallas_call | solution.py:286
  28.8 0.9 %shard_map.60 = (f32[224,896]{1,0:T(8,128)}, f32[896]{0:T(1024)}) custom-call(f32[224,896]{1,0:T(8,128)S(1)} %get-tuple-element.6.gram_ref, f32[8,128]{1,0:T(8,128)S(1)} %get-tuple-element.7.rhs_ref), custom_call_target="tpu_custom_call" | custom-call | tf_op jit(solution)/shard_map/pallas_call | solution.py:317

commit v2 on v0

v2 whole, which is shorter than its diff:
```python
import functools
import math

import jax
import jax.numpy as jnp
from jax import lax
from jax.experimental import pallas as pl
from jax.experimental.pallas import tpu as pltpu
from jax.sharding import PartitionSpec as P

MESH = pl.DeviceIdType.MESH
BASE = 256


def up(n, m):
    return -(-n // m) * m


class Plan:
    def __init__(self, nin):
        self.nin = nin
        self.half = nin // 2
        self.single = up(nin + 1, 8)
        self.slab = up(nin + 2, 8)
        self.q2 = self.single
        self.q3 = self.single + nin
        self.rows_a = max(up(self.single + 2 * nin, 16), 64)
        self.low = self.single
        self.high = self.low + self.half * (self.half - 1) // 2
        rest = nin - self.half
        self.rows_b = max(up(self.high + rest * (rest - 1) // 2, 16), 128)


def positions(plan, degrees):
    total = jnp.zeros_like(degrees[0:1, :])
    first, second, third = total, total, total
    for j in range(plan.nin):
        total = total + degrees[j : j + 1, :]
        first = first + (total < 1).astype(jnp.int32)
        second = second + (total < 2).astype(jnp.int32)
        third = third + (total < 3).astype(jnp.int32)
    nin, half = plan.nin, plan.half
    low = second < half
    big = jnp.where(low, second, third - half)
    small = jnp.where(low, first, second - half)
    pair = jnp.where(low, plan.low, plan.high) + (big * (big - 1)) // 2 + small
    a = jnp.where(low, third, first)
    b = pair
    twin = (first == second) | (second == third)
    a = jnp.where(twin, plan.q2 + second, a)
    b = jnp.where(twin, jnp.where(first == second, third, first), b)
    triple = (first == second) & (second == third)
    a = jnp.where(triple, plan.q3 + first, a)
    b = jnp.where(triple, nin, b)
    a = jnp.where((third == nin) & (first != second), first, a)
    b = jnp.where((third == nin) & (first != second), second, b)
    a = jnp.where(first == nin, nin, a)
    b = jnp.where(first == nin, nin, b)
    return a * BASE + b


def split(v):
    high = v.astype(jnp.bfloat16)
    return high, (v - high.astype(jnp.float32)).astype(jnp.bfloat16)


def build_tables(plan, samples_total, slab, work, ta, tb, z_ref):
    nin, single = plan.nin, plan.single
    x = slab[0:single, :]
    weights = slab[nin : nin + 1, :]
    root = jnp.sqrt(weights / samples_total)
    scaled = weights * slab[nin + 1 : nin + 2, :] / samples_total
    z_high, z_low = split(scaled.astype(jnp.bfloat16).astype(jnp.float32) / root)
    z_ref[...] = jnp.concatenate(
        [z_high.astype(jnp.float32), z_low.astype(jnp.float32), jnp.zeros((14, x.shape[1]), jnp.float32)], axis=0
    ).astype(jnp.bfloat16)
    rows = lax.broadcasted_iota(jnp.int32, x.shape, 0)
    q1 = jnp.where(rows < nin, math.sqrt(3.0) * x, (rows == nin).astype(jnp.float32))
    q2 = math.sqrt(5.0) * (1.5 * x * x - 0.5) * root
    q3 = math.sqrt(7.0) * (2.5 * x * x * x - 1.5 * x) * root
    parts = [q1 * root, q2[0:nin, :], q3[0:nin, :]]
    spare = plan.rows_a - plan.q3 - nin
    if spare:
        parts.append(jnp.zeros((spare, x.shape[1]), jnp.float32))
    ta[0 : plan.rows_a, :], ta[plan.rows_a : 2 * plan.rows_a, :] = split(jnp.concatenate(parts, axis=0))
    work[0:single, :] = q1
    for begin, end, base in ((0, plan.half, plan.low), (plan.half, nin, plan.high)):
        for b in range(1, end - begin):
            at = base + b * (b - 1) // 2
            work[at : at + b, :] = q1[begin : begin + b, :] * q1[begin + b : begin + b + 1, :]
    tb[0 : plan.rows_b, :], tb[plan.rows_b : 2 * plan.rows_b, :] = split(work[...])


def xor_index(a, b, n):
    if n & (n - 1):
        return lax.rem(a + b, n)
    out, bit = 0, 1
    while bit < n:
        out = out + bit * (((a // bit) % 2 + (b // bit) % 2) % 2)
        bit *= 2
    return out


def kernel(
    plan, sizes, columns, samples_total,
    x_hbm, w_hbm, y_hbm, deg_hbm, acc,
    slabs, x_ref, w_ref, y_ref, deg_ref, codes_in, sel_a, sel_b, ta0, tb0, z0, ta1, tb1, z1, work0, work1, d0, d1,
    load_sem, ici_send, sub_send, recv, code_send, code_recv,
):
    nsmp, nsub, ntrm = sizes
    smp, sub, trm = lax.axis_index("smp"), lax.axis_index("sub"), lax.axis_index("trm")
    me = smp * nsub + sub
    nin = plan.nin
    terms = deg_ref.shape[1]
    width = codes_in.shape[2]
    right = up(columns, 16)

    barrier = pltpu.get_barrier_semaphore()
    for d in range(1, nsmp):
        pl.semaphore_signal(barrier, inc=1, device_id={"smp": xor_index(smp, d, nsmp)}, device_id_type=MESH)
    for d in range(1, nsub):
        pl.semaphore_signal(barrier, inc=1, device_id={"sub": lax.rem(sub + d, nsub)}, device_id_type=MESH)
    for d in range(1, ntrm):
        pl.semaphore_signal(barrier, inc=1, device_id={"trm": lax.rem(trm + d, ntrm)}, device_id_type=MESH)

    mine = slabs.at[me]
    loads = [
        pltpu.make_async_copy(deg_hbm, deg_ref, load_sem.at[0]),
        pltpu.make_async_copy(x_hbm, x_ref, load_sem.at[1]),
        pltpu.make_async_copy(w_hbm, w_ref, load_sem.at[2]),
        pltpu.make_async_copy(y_hbm, y_ref, load_sem.at[3]),
    ]
    for load in loads:
        load.start()
    work0[...] = jnp.zeros_like(work0)
    work1[...] = jnp.zeros_like(work1)
    acc[...] = jnp.zeros_like(acc)
    for load in loads[1:]:
        load.wait()
    spare = plan.slab - nin - 2
    mine[...] = jnp.concatenate(
        [x_ref[...], w_ref[...], y_ref[...], jnp.zeros((spare, x_ref.shape[1]), jnp.float32)], axis=0
    )
    loads[0].wait()
    code = positions(plan, deg_ref[...])
    per_trm = terms // columns
    for k in range(per_trm):
        @pl.when(lax.rem(me, per_trm) == k)
        def _():
            part = code[:, k * columns : (k + 1) * columns].astype(jnp.float32)
            pad = jnp.full((1, width - columns), -1.0, jnp.float32)
            codes_in[trm] = jnp.broadcast_to(jnp.concatenate([part, pad], axis=1), (8, width))

    pl.semaphore_wait(barrier, (nsmp - 1) + (nsub - 1) + (ntrm - 1))

    def sub_copy(chunk, p, d):
        return pltpu.make_async_remote_copy(
            src_ref=slabs.at[chunk], dst_ref=slabs.at[chunk],
            send_sem=sub_send.at[p, d - 1], recv_sem=recv.at[chunk],
            device_id={"sub": lax.rem(sub + d, nsub)}, device_id_type=MESH,
        )

    def ici_copy(d):
        return pltpu.make_async_remote_copy(
            src_ref=slabs.at[me], dst_ref=slabs.at[me],
            send_sem=ici_send.at[d - 1], recv_sem=recv.at[me],
            device_id={"smp": xor_index(smp, d, nsmp)}, device_id_type=MESH,
        )

    def code_copy(d):
        return pltpu.make_async_remote_copy(
            src_ref=codes_in.at[trm], dst_ref=codes_in.at[trm],
            send_sem=code_send.at[d - 1], recv_sem=code_recv.at[trm],
            device_id={"trm": lax.rem(trm + d, ntrm)}, device_id_type=MESH,
        )

    def wait_slab(chunk):
        pltpu.make_async_remote_copy(
            src_ref=slabs.at[chunk], dst_ref=slabs.at[chunk],
            send_sem=ici_send.at[0], recv_sem=recv.at[chunk],
            device_id={"sub": lax.rem(sub + 1, nsub)}, device_id_type=MESH,
        ).wait_recv()

    for d in range(1, nsmp):
        ici_copy(d).start()
    for d in range(1, nsub):
        sub_copy(me, 0, d).start()
    for d in range(1, ntrm):
        code_copy(d).start()

    build_tables(plan, samples_total, slabs[me], work0, ta0, tb0, z0)

    def select(row, base, count, limit):
        column = jnp.broadcast_to(row, (128, 128)).T.astype(jnp.int32)[0:count, :]
        for ref, wanted, rows in ((sel_a, column >> 8, plan.rows_a), (sel_b, column & (BASE - 1), plan.rows_b)):
            for j in range(0, ref.shape[1], 128):
                lane = lax.rem(lax.broadcasted_iota(jnp.int32, (count, 128), 1) + j, rows)
                ref[base : base + count, j : j + 128] = (wanted == lane).astype(jnp.bfloat16)

    for i in range(0, terms, 128):
        count = min(128, terms - i)
        row = code[:, i : i + count].astype(jnp.float32)
        if count < 128:
            row = jnp.concatenate([row, jnp.zeros((1, 128 - count), jnp.float32)], axis=1)
        select(row, i, count, terms)

    for d in range(1, ntrm):
        other = lax.rem(trm + d, ntrm)
        pltpu.make_async_remote_copy(
            src_ref=codes_in.at[other], dst_ref=codes_in.at[other],
            send_sem=code_send.at[d - 1], recv_sem=code_recv.at[other],
            device_id={"trm": other}, device_id_type=MESH,
        ).wait_recv()
    wanted = codes_in[me // per_trm]
    for i in range(0, right, 128):
        select(wanted[0:1, i : i + 128], terms + i, min(128, right - i), right)

    def chunk_of(p, s):
        return xor_index(smp, p, nsmp) * nsub + lax.rem(sub + s, nsub)

    def compute(ta, tb, z_ref, d_ref):
        dims = (((1,), (0,)), ((), ()))
        selected = terms + right
        for n in range(0, d_ref.shape[1], 256):
            a = lax.dot_general(sel_a[...], ta[:, n : n + 256], dims, preferred_element_type=jnp.float32)
            b = lax.dot_general(sel_b[...], tb[:, n : n + 256], dims, preferred_element_type=jnp.float32)
            d_ref[0:selected, n : n + 256] = (a * b).astype(jnp.bfloat16)
        d_ref[selected : selected + 16, :] = z_ref[...]
        for c in range(0, terms, 256):
            e = min(c + 256, terms)
            acc[:, c:e] += lax.dot_general(
                d_ref[terms : selected + 16, :], d_ref[c:e, :], (((1,), (1,)), ((), ())),
                preferred_element_type=jnp.float32,
            )

    def body(p, carry):
        second = chunk_of(p, 1)
        wait_slab(second)
        compute(ta0, tb0, z0, d0)
        build_tables(plan, samples_total, slabs[second], work1, ta1, tb1, z1)
        following = chunk_of(lax.rem(p + 1, nsmp), 0)

        @pl.when(p + 1 < nsmp)
        def _():
            wait_slab(following)
            for d in range(1, nsub):
                sub_copy(following, p + 1, d).start()

        compute(ta1, tb1, z1, d1)
        build_tables(plan, samples_total, slabs[following], work0, ta0, tb0, z0)
        return carry

    lax.fori_loop(0, nsmp, body, 0)

    for d in range(1, ntrm):
        code_copy(d).wait_send()
    for d in range(1, nsmp):
        ici_copy(d).wait_send()
    for p in range(nsmp):
        for d in range(1, nsub):
            sub_copy(chunk_of(p, 0), p, d).wait_send()


def write_out(columns, acc_ref, gram_out, rhs_out, flat, sem):
    copy = pltpu.make_async_copy(acc_ref.at[0 : gram_out.shape[0], :], gram_out, sem.at[0])
    copy.start()
    z = up(columns, 16)
    terms = acc_ref.shape[1]
    line = acc_ref[z : z + 1, :] + acc_ref[z + 1 : z + 2, :]
    line = jnp.concatenate([line, jnp.zeros((1, flat.shape[0] - terms), jnp.float32)], axis=1)
    rows = [line[:, i : i + 128] for i in range(0, flat.shape[0], 128)]
    flat[...] = jnp.concatenate(rows, axis=0).reshape(flat.shape)
    tail = pltpu.make_async_copy(flat.at[pl.ds(0, rhs_out.shape[0])], rhs_out, sem.at[1])
    tail.start()
    tail.wait()
    copy.wait()


def solution(mesh):
    nsmp, nsub, ntrm = mesh.shape["smp"], mesh.shape["sub"], mesh.shape["trm"]

    def local(inputs, weights, response, index_table):
        nin, samples = inputs.shape
        terms = index_table.shape[1]
        columns = terms * ntrm // (nsmp * nsub)
        plan = Plan(nin)
        right = up(columns, 16)
        width = up(columns, 128)
        chunks = nsmp * nsub
        acc = pl.pallas_call(
            functools.partial(kernel, plan, (nsmp, nsub, ntrm), columns, samples * chunks),
            out_shape=pltpu.VMEM((right + 16, terms), jnp.float32),
            in_specs=[pl.BlockSpec(memory_space=pltpu.HBM)] * 4,
            out_specs=pl.BlockSpec(memory_space=pltpu.VMEM),
            scratch_shapes=[
                pltpu.VMEM((chunks, plan.slab, samples), jnp.float32),
                pltpu.VMEM((nin, samples), jnp.float32),
                pltpu.VMEM((1, samples), jnp.float32),
                pltpu.VMEM((1, samples), jnp.float32),
                pltpu.VMEM((nin, terms), jnp.int32),
                pltpu.VMEM((ntrm, 8, width), jnp.float32),
                pltpu.VMEM((terms + right, 2 * plan.rows_a), jnp.bfloat16),
                pltpu.VMEM((terms + right, 2 * plan.rows_b), jnp.bfloat16),
            ]
            + [
                pltpu.VMEM((2 * plan.rows_a, samples), jnp.bfloat16),
                pltpu.VMEM((2 * plan.rows_b, samples), jnp.bfloat16),
                pltpu.VMEM((16, samples), jnp.bfloat16),
            ]
            * 2
            + [pltpu.VMEM((plan.rows_b, samples), jnp.float32)] * 2
            + [pltpu.VMEM((terms + right + 16, samples), jnp.bfloat16)] * 2
            + [
                pltpu.SemaphoreType.DMA((4,)),
                pltpu.SemaphoreType.DMA((max(nsmp - 1, 1),)),
                pltpu.SemaphoreType.DMA((nsmp, max(nsub - 1, 1))),
                pltpu.SemaphoreType.DMA((chunks,)),
                pltpu.SemaphoreType.DMA((max(ntrm - 1, 1),)),
                pltpu.SemaphoreType.DMA((ntrm,)),
            ],
            compiler_params=pltpu.CompilerParams(
                collective_id=0, has_side_effects=True, vmem_limit_bytes=40 * 1024 * 1024
            ),
        )(*map(
            lambda v: pltpu.with_memory_space_constraint(v, pltpu.HBM),
            (inputs, weights.reshape(1, samples), response.reshape(1, samples), index_table),
        ))
        gram, rhs = pl.pallas_call(
            functools.partial(write_out, columns),
            out_shape=(
                jax.ShapeDtypeStruct((up(columns, 8), terms), jnp.float32),
                jax.ShapeDtypeStruct((up(terms, 1024) if terms % 128 else terms,), jnp.float32),
            ),
            in_specs=[pl.BlockSpec(memory_space=pltpu.VMEM)],
            out_specs=(pl.BlockSpec(memory_space=pl.ANY),) * 2,
            scratch_shapes=[
                pltpu.VMEM((up(terms, 1024),), jnp.float32),
                pltpu.SemaphoreType.DMA((2,)),
            ],
        )(pltpu.with_memory_space_constraint(acc, pltpu.VMEM))
        return gram[0:columns].T, rhs[0:terms]

    return jax.shard_map(
        local,
        mesh=mesh,
        in_specs=(
            P(None, ("grp", "smp", "sub")),
            P(("grp", "smp", "sub")),
            P(("grp", "smp", "sub")),
            P(None, "trm"),
        ),
        out_specs=(P(("grp", "trm"), ("smp", "sub")), P(("grp", "trm"))),
        check_vma=False,
    )
```

time: 33.2 us -> 18.4 us (0.55)
  Pallas kernels: 29 us -> 17.6 us
  local copies, waits for them, and re-layouts: 2.74 us -> 0 us
  other arithmetic: 0.61 us -> 0 us
    pallas_call x1, Pallas kernels: 29 us -> 16.7 us  [local(): pl.pallas_call(functools.partial(kernel, plan, (nsmp, nsub, ntrm), column...]
    unnamed x3 -> x0, local copies, waits for them, and re-layouts: 2.74 us -> none
    pallas_call x0 -> x1, Pallas kernels: none -> 0.9 us  [local(): pl.pallas_call(functools.partial(write_out, columns), out_shape=(jax.Shap...]
    pallas_call x1 -> x0, other arithmetic: 0.61 us -> none  [local(): pl.pallas_call(functools.partial(kernel, plan, (nsmp, nsub, ntrm), column...]
where the time goes in v2:
time: 18.4 us; the launch traced here: 18.3 us
  Pallas kernels  17.6 us (96%)
  between operations  0.64 us (3%)
    pallas_call x1, Pallas kernels, local(): pl.pallas_call(functools.partial(kernel, plan, (nsmp, nsub, ntrm), column...  16.7 us
    pallas_call x1, Pallas kernels, local(): pl.pallas_call(functools.partial(write_out, columns), out_shape=(jax.Shap...  0.9 us

profile of v2, /device:TPU:0, one launch (start us, length us, event | category | flops | bytes accessed | tf_op | source)
XLA Modules:
  0.0 18.3 jit_solution(8967143567442148086)
XLA Ops:
  0.6 16.7 %shard_map.59.acc_ref = f32[240,896]{1,0:T(8,128)S(1)} custom-call(f32[20,512]{1,0:T(8,128)} %x_hbm.1, f32[1,512]{1,0:T(1,128)} %bitcast.3, f32[1,512]{1,0:T(1,128)} %bitcast.4, s32[20,896]{1,0:T(8,128)} %deg_hbm.1), custom_call_target="tpu_custom_call" | custom-call | tf_op jit(solution)/shard_map/pallas_call | solution.py:290
  17.4 0.9 %shard_map.60 = (f32[224,896]{1,0:T(8,128)}, f32[896]{0:T(1024)}) custom-call(f32[240,896]{1,0:T(8,128)S(1)} %shard_map.59.acc_ref), custom_call_target="tpu_custom_call" | custom-call | tf_op jit(solution)/shard_map/pallas_call | solution.py:328

commit v3 on v2

--- a/solution.py
+++ b/solution.py
@@ -32,13 +32,16 @@
 
 
 def positions(plan, degrees):
-    total = jnp.zeros_like(degrees[0:1, :])
-    first, second, third = total, total, total
-    for j in range(plan.nin):
-        total = total + degrees[j : j + 1, :]
-        first = first + (total < 1).astype(jnp.int32)
-        second = second + (total < 2).astype(jnp.int32)
-        third = third + (total < 3).astype(jnp.int32)
+    degrees = degrees.astype(jnp.float32)
+    index = lax.broadcasted_iota(jnp.int32, degrees.shape, 0).astype(jnp.float32)
+    present = degrees > 0
+    total = jnp.sum(degrees, axis=0, keepdims=True)
+    weighted = jnp.sum(degrees * index, axis=0, keepdims=True).astype(jnp.int32)
+    least = jnp.min(jnp.where(present, index, plan.nin), axis=0, keepdims=True).astype(jnp.int32)
+    most = jnp.max(jnp.where(present, index, -1), axis=0, keepdims=True).astype(jnp.int32)
+    first = least
+    second = jnp.where(total > 2, weighted - least - most, jnp.where(total > 1, most, plan.nin))
+    third = jnp.where(total > 2, most, plan.nin)
     nin, half = plan.nin, plan.half
     low = second < half
     big = jnp.where(low, second, third - half)
@@ -114,6 +117,7 @@
     terms = deg_ref.shape[1]
     width = codes_in.shape[2]
     right = up(columns, 16)
+    selected = terms + right
 
     barrier = pltpu.get_barrier_semaphore()
     for d in range(1, nsmp):
@@ -188,9 +192,41 @@
     for d in range(1, ntrm):
         code_copy(d).start()
 
-    build_tables(plan, samples_total, slabs[me], work0, ta0, tb0, z0)
-
-    def select(row, base, count, limit):
+    def chunk_of(p, s):
+        return xor_index(smp, p, nsmp) * nsub + lax.rem(sub + s, nsub)
+
+    def pick(ta, tb, d_ref, begin, end):
+        dims = (((1,), (0,)), ((), ()))
+        for n in range(0, d_ref.shape[1], 256):
+            a = lax.dot_general(sel_a[begin:end, :], ta[:, n : n + 256], dims, preferred_element_type=jnp.float32)
+            b = lax.dot_general(sel_b[begin:end, :], tb[:, n : n + 256], dims, preferred_element_type=jnp.float32)
+            d_ref[begin:end, n : n + 256] = (a * b).astype(jnp.bfloat16)
+
+    def add(z_ref, d_ref):
+        d_ref[selected : selected + 16, :] = z_ref[...]
+        for c in range(0, terms, 256):
+            e = min(c + 256, terms)
+            acc[:, c:e] += lax.dot_general(
+                d_ref[terms : selected + 16, :], d_ref[c:e, :], (((1,), (1,)), ((), ())),
+                preferred_element_type=jnp.float32,
+            )
+
+    def next_own(p):
+        following = chunk_of(lax.rem(p + 1, nsmp), 0)
+
+        @pl.when(p + 1 < nsmp)
+        def _():
+            wait_slab(following)
+            for d in range(1, nsub):
+                sub_copy(following, p + 1, d).start()
+
+        return slabs[following]
+
+    set0, set1 = (work0, ta0, tb0, z0), (work1, ta1, tb1, z1)
+
+    build_tables(plan, samples_total, slabs[me], *set0)
+
+    def select(row, base, count):
         column = jnp.broadcast_to(row, (128, 128)).T.astype(jnp.int32)[0:count, :]
         for ref, wanted, rows in ((sel_a, column >> 8, plan.rows_a), (sel_b, column & (BASE - 1), plan.rows_b)):
             for j in range(0, ref.shape[1], 128):
@@ -202,7 +238,13 @@
         row = code[:, i : i + count].astype(jnp.float32)
         if count < 128:
             row = jnp.concatenate([row, jnp.zeros((1, 128 - count), jnp.float32)], axis=1)
-        select(row, i, count, terms)
+        select(row, i, count)
+
+    partner = chunk_of(0, 1)
+    pick(ta0, tb0, d0, 0, terms)
+    wait_slab(partner)
+    build_tables(plan, samples_total, slabs[partner], *set1)
+    pick(ta1, tb1, d1, 0, terms)
 
     for d in range(1, ntrm):
         other = lax.rem(trm + d, ntrm)
@@ -213,44 +255,28 @@
         ).wait_recv()
     wanted = codes_in[me // per_trm]
     for i in range(0, right, 128):
-        select(wanted[0:1, i : i + 128], terms + i, min(128, right - i), right)
-
-    def chunk_of(p, s):
-        return xor_index(smp, p, nsmp) * nsub + lax.rem(sub + s, nsub)
-
-    def compute(ta, tb, z_ref, d_ref):
-        dims = (((1,), (0,)), ((), ()))
-        selected = terms + right
-        for n in range(0, d_ref.shape[1], 256):
-            a = lax.dot_general(sel_a[...], ta[:, n : n + 256], dims, preferred_element_type=jnp.float32)
-            b = lax.dot_general(sel_b[...], tb[:, n : n + 256], dims, preferred_element_type=jnp.float32)
-            d_ref[0:selected, n : n + 256] = (a * b).astype(jnp.bfloat16)
-        d_ref[selected : selected + 16, :] = z_ref[...]
-        for c in range(0, terms, 256):
-            e = min(c + 256, terms)
-            acc[:, c:e] += lax.dot_general(
-                d_ref[terms : selected + 16, :], d_ref[c:e, :], (((1,), (1,)), ((), ())),
-                preferred_element_type=jnp.float32,
-            )
+        select(wanted[0:1, i : i + 128], terms + i, min(128, right - i))
+    pick(ta0, tb0, d0, terms, selected)
+
+    add(z0, d0)
+    following = next_own(0)
+    pick(ta1, tb1, d1, terms, selected)
+    add(z1, d1)
+    build_tables(plan, samples_total, following, *set0)
 
     def body(p, carry):
         second = chunk_of(p, 1)
         wait_slab(second)
-        compute(ta0, tb0, z0, d0)
-        build_tables(plan, samples_total, slabs[second], work1, ta1, tb1, z1)
-        following = chunk_of(lax.rem(p + 1, nsmp), 0)
-
-        @pl.when(p + 1 < nsmp)
-        def _():
-            wait_slab(following)
-            for d in range(1, nsub):
-                sub_copy(following, p + 1, d).start()
-
-        compute(ta1, tb1, z1, d1)
-        build_tables(plan, samples_total, slabs[following], work0, ta0, tb0, z0)
+        pick(ta0, tb0, d0, 0, selected)
+        add(z0, d0)
+        build_tables(plan, samples_total, slabs[second], *set1)
+        following = next_own(p)
+        pick(ta1, tb1, d1, 0, selected)
+        add(z1, d1)
+        build_tables(plan, samples_total, following, *set0)
         return carry
 
-    lax.fori_loop(0, nsmp, body, 0)
+    lax.fori_loop(1, nsmp, body, 0)
 
     for d in range(1, ntrm):
         code_copy(d).wait_send()

time: 18.4 us -> 17.7 us (0.962)
  Pallas kernels: 17.6 us -> 16.9 us
    pallas_call x1, Pallas kernels: 16.7 us -> 16 us  [local(): pl.pallas_call(functools.partial(kernel, plan, (nsmp, nsub, ntrm), column...]
where the time goes in v3:
time: 17.7 us; the launch traced here: 17.5 us
  Pallas kernels  16.9 us (95%)
  between operations  0.64 us (4%)
    pallas_call x1, Pallas kernels, local(): pl.pallas_call(functools.partial(kernel, plan, (nsmp, nsub, ntrm), column...  16 us
    pallas_call x1, Pallas kernels, local(): pl.pallas_call(functools.partial(write_out, columns), out_shape=(jax.Shap...  0.9 us

profile of v3, /device:TPU:0, one launch (start us, length us, event | category | flops | bytes accessed | tf_op | source)
XLA Modules:
  0.0 17.5 jit_solution(2520904356066975759)
XLA Ops:
  0.6 16.0 %shard_map.59.acc_ref = f32[240,896]{1,0:T(8,128)S(1)} custom-call(f32[20,512]{1,0:T(8,128)} %x_hbm.1, f32[1,512]{1,0:T(1,128)} %bitcast.3, f32[1,512]{1,0:T(1,128)} %bitcast.4, s32[20,896]{1,0:T(8,128)} %deg_hbm.1), custom_call_target="tpu_custom_call" | custom-call | tf_op jit(solution)/shard_map/pallas_call | solution.py:316
  16.6 0.9 %shard_map.60 = (f32[224,896]{1,0:T(8,128)}, f32[896]{0:T(1024)}) custom-call(f32[240,896]{1,0:T(8,128)S(1)} %shard_map.59.acc_ref), custom_call_target="tpu_custom_call" | custom-call | tf_op jit(solution)/shard_map/pallas_call | solution.py:354

commit v4 on v3

--- a/solution.py
+++ b/solution.py
@@ -10,6 +10,8 @@
 
 MESH = pl.DeviceIdType.MESH
 BASE = 256
+SCALE_X = 32767.0
+SCALE_W = 8191.0
 
 
 def up(n, m):
@@ -21,7 +23,7 @@
         self.nin = nin
         self.half = nin // 2
         self.single = up(nin + 1, 8)
-        self.slab = up(nin + 2, 8)
+        self.groups = -(-(nin + 4) // 8)
         self.q2 = self.single
         self.q3 = self.single + nin
         self.rows_a = max(up(self.single + 2 * nin, 16), 64)
@@ -67,18 +69,52 @@
     return high, (v - high.astype(jnp.float32)).astype(jnp.bfloat16)
 
 
+def coarse_fine(v):
+    v = v * SCALE_W
+    coarse = jnp.round(v)
+    return [coarse, jnp.round((v - coarse) * (2.0 * SCALE_X))]
+
+
+def encode(plan, x, weights, response):
+    rows = [jnp.round(x * SCALE_X)] + coarse_fine(weights) + coarse_fine(response)
+    spare = 8 * plan.groups - plan.nin - 4
+    if spare:
+        rows.append(jnp.zeros((spare, x.shape[1]), jnp.float32))
+    rows = jnp.concatenate(rows, axis=0).astype(jnp.int32)
+    half = x.shape[1] // 2
+    parts = []
+    for g in range(plan.groups):
+        group = rows[8 * g : 8 * g + 8, :]
+        parts.append(jnp.concatenate([group[:, 0:half], group[:, half:]], axis=0))
+    return jnp.concatenate(parts, axis=1).astype(jnp.int16)
+
+
+def decode(plan, slab):
+    half = slab.shape[1] // plan.groups
+    parts = []
+    for g in range(plan.groups):
+        group = slab[:, g * half : (g + 1) * half].astype(jnp.int32).astype(jnp.float32)
+        parts.append(jnp.concatenate([group[0:8, :], group[8:16, :]], axis=1))
+    return jnp.concatenate(parts, axis=0)
+
+
 def build_tables(plan, samples_total, slab, work, ta, tb, z_ref):
     nin, single = plan.nin, plan.single
-    x = slab[0:single, :]
-    weights = slab[nin : nin + 1, :]
+    rows = decode(plan, slab)
+
+    def joined(i):
+        return (rows[i : i + 1, :] + rows[i + 1 : i + 2, :] * (0.5 / SCALE_X)) * (1.0 / SCALE_W)
+
+    x = rows[0:single, :] * (1.0 / SCALE_X)
+    weights = joined(nin)
     root = jnp.sqrt(weights / samples_total)
-    scaled = weights * slab[nin + 1 : nin + 2, :] / samples_total
+    scaled = weights * joined(nin + 2) / samples_total
     z_high, z_low = split(scaled.astype(jnp.bfloat16).astype(jnp.float32) / root)
     z_ref[...] = jnp.concatenate(
         [z_high.astype(jnp.float32), z_low.astype(jnp.float32), jnp.zeros((14, x.shape[1]), jnp.float32)], axis=0
     ).astype(jnp.bfloat16)
-    rows = lax.broadcasted_iota(jnp.int32, x.shape, 0)
-    q1 = jnp.where(rows < nin, math.sqrt(3.0) * x, (rows == nin).astype(jnp.float32))
+    index = lax.broadcasted_iota(jnp.int32, x.shape, 0)
+    q1 = jnp.where(index < nin, math.sqrt(3.0) * x, (index == nin).astype(jnp.float32))
     q2 = math.sqrt(5.0) * (1.5 * x * x - 0.5) * root
     q3 = math.sqrt(7.0) * (2.5 * x * x * x - 1.5 * x) * root
     parts = [q1 * root, q2[0:nin, :], q3[0:nin, :]]
@@ -141,10 +177,7 @@
     acc[...] = jnp.zeros_like(acc)
     for load in loads[1:]:
         load.wait()
-    spare = plan.slab - nin - 2
-    mine[...] = jnp.concatenate(
-        [x_ref[...], w_ref[...], y_ref[...], jnp.zeros((spare, x_ref.shape[1]), jnp.float32)], axis=0
-    )
+    mine[...] = encode(plan, x_ref[...], w_ref[...], y_ref[...])
     loads[0].wait()
     code = positions(plan, deg_ref[...])
     per_trm = terms // columns
@@ -319,7 +352,7 @@
             in_specs=[pl.BlockSpec(memory_space=pltpu.HBM)] * 4,
             out_specs=pl.BlockSpec(memory_space=pltpu.VMEM),
             scratch_shapes=[
-                pltpu.VMEM((chunks, plan.slab, samples), jnp.float32),
+                pltpu.VMEM((chunks, 16, plan.groups * samples // 2), jnp.int16),
                 pltpu.VMEM((nin, samples), jnp.float32),
                 pltpu.VMEM((1, samples), jnp.float32),
                 pltpu.VMEM((1, samples), jnp.float32),

time: 17.7 us -> 17.6 us (level)
  no operation moved by 1% of the time
where the time goes in v4:
time: 17.6 us; the launch traced here: 17.5 us
  Pallas kernels  16.8 us (95%)
  between operations  0.64 us (4%)
    pallas_call x1, Pallas kernels, local(): pl.pallas_call(functools.partial(kernel, plan, (nsmp, nsub, ntrm), column...  15.9 us
    pallas_call x1, Pallas kernels, local(): pl.pallas_call(functools.partial(write_out, columns), out_shape=(jax.Shap...  0.9 us

profile of v4, /device:TPU:0, one launch (start us, length us, event | category | flops | bytes accessed | tf_op | source)
XLA Modules:
  0.0 17.5 jit_solution(9014160560723776409)
XLA Ops:
  0.6 15.9 %shard_map.59.acc_ref = f32[240,896]{1,0:T(8,128)S(1)} custom-call(f32[20,512]{1,0:T(8,128)} %x_hbm.1, f32[1,512]{1,0:T(1,128)} %bitcast.3, f32[1,512]{1,0:T(1,128)} %bitcast.4, s32[20,896]{1,0:T(8,128)} %deg_hbm.1), custom_call_target="tpu_custom_call" | custom-call | tf_op jit(solution)/shard_map/pallas_call | solution.py:349
  16.6 0.9 %shard_map.60 = (f32[224,896]{1,0:T(8,128)}, f32[896]{0:T(1024)}) custom-call(f32[240,896]{1,0:T(8,128)S(1)} %shard_map.59.acc_ref), custom_call_target="tpu_custom_call" | custom-call | tf_op jit(solution)/shard_map/pallas_call | solution.py:387
